TPU v7x, 32 devices: a whole 2x2x4 slice. The times are simulated.
32 devices in a mesh: layer: 2 (over x), blk: 16 (over z, y, core).
Axes of the slice: x: 2, y: 2, z: 4, core: 2. Of those that a mesh axis runs over, the one named last changes fastest.
Arguments:
- points: bfloat16 [12288, 256], P('blk'), may hold values from -8.4 to 8.4
- labels: int32 [12288], P('blk'), may hold values from 0 to 255, as said below
Outputs:
- distance: float32 [12288, 256], P('blk')
Inputs may be any that keep to these rules, and one draw needn't show every extreme that they name: `labels`: every cluster is named by at least one point.
All inputs are finite; a program needn't handle non-finite values.
Results may differ from a plain program's by a relative error of at most 0.00034.
Values may be sent and summed in bfloat16 or wider, within the bound.
A program may use at most 64 MiB of HBM per device.

v0:
```python
import jax
import jax.numpy as jnp
from jax import lax
from jax.sharding import PartitionSpec as P

K = 256


def as_sent(x):
    return jax.tree.map(lambda a: a.astype(jnp.bfloat16) if a.dtype == jnp.float32 else a, x)


def from_behind(x, axis, by):
    devices = lax.axis_size(axis)
    return lax.ppermute(x, axis, [(i, (i + by) % devices) for i in range(devices)])


def choose_where(chosen, shifted, carried):
    return tuple(
        (jnp.where(chosen, new_part, old_part) for new_part, old_part in zip(shifted, carried))
    )


def shards(points, labels):
    feature_width = points.shape[1]
    own_rows = points.shape[0]
    layers = lax.axis_size("layer")
    blocks = lax.axis_size("blk")
    visit_count = blocks // layers
    half_steps = visit_count // 2
    layer_idx = lax.axis_index("layer")
    offset_bits = (layers - 1).bit_length()
    own_sq = jnp.sum(jnp.square(points.astype(jnp.float32)), axis=1)
    cluster_ids = jnp.arange(K, dtype=jnp.float32)
    tagged = labels.astype(jnp.bfloat16)

    def accumulate(partial_value, visiting, block_tags):
        visit_sq = jnp.sum(jnp.square(visiting.astype(jnp.float32)), axis=1)
        gram_block = lax.dot_general(
            points, visiting, (((1,), (1,)), ((), ())), preferred_element_type=jnp.float32
        )
        kernel = jnp.exp(
            -(own_sq[:, None] + visit_sq[None, :] - 2.0 * gram_block) / feature_width
        ).astype(jnp.bfloat16)
        onehot = (block_tags.astype(jnp.float32)[:, None] == cluster_ids[None, :]).astype(
            jnp.bfloat16
        )
        return partial_value + jnp.dot(kernel, onehot, preferred_element_type=jnp.float32)

    initial = jnp.zeros((own_rows, K), jnp.float32)
    carried = (points, tagged)
    for bit_pos in range(offset_bits):
        shifted = jax.tree.map(
            lambda part, own: part.astype(own.dtype),
            from_behind(as_sent(carried), "blk", visit_count << bit_pos),
            carried,
        )
        carried = choose_where(layer_idx >> bit_pos & 1 == 1, shifted, carried)
    climbing = jax.tree.map(
        lambda part, own: part.astype(own.dtype),
        from_behind(as_sent(carried), "blk", half_steps),
        carried,
    )
    falling = jax.tree.map(
        lambda part, own: part.astype(own.dtype),
        from_behind(as_sent(carried), "blk", half_steps - 1),
        carried,
    )
    partial_value = accumulate(
        accumulate(initial, climbing[0], climbing[1]), falling[0], falling[1]
    )

    def split_turn(turn_index, loop_state):
        partial_now, climb_pts, climb_tags, fall_pts, fall_tags = loop_state
        climb_pts, climb_tags = from_behind((climb_pts, climb_tags), "blk", 1)
        fall_pts, fall_tags = from_behind((fall_pts, fall_tags), "blk", -1)
        partial_now = accumulate(partial_now, climb_pts, climb_tags)
        partial_now = accumulate(partial_now, fall_pts, fall_tags)
        return (partial_now, climb_pts, climb_tags, fall_pts, fall_tags)

    partial_value = lax.fori_loop(
        0,
        half_steps - 1,
        split_turn,
        (partial_value, climbing[0], climbing[1], falling[0], falling[1]),
    )[0]
    row_sums = lax.psum(partial_value, "layer")
    member_f = (labels[:, None] == jnp.arange(K, dtype=jnp.int32)[None, :]).astype(jnp.float32)
    within, counts = lax.psum(
        (jnp.sum(member_f * row_sums, axis=0), jnp.sum(member_f, axis=0)), "blk"
    )
    distance = 1.0 - 2.0 * row_sums / counts[None, :] + within[None, :] / (counts * counts)[None, :]
    return distance


def solution(mesh):
    in_specs = (P("blk", None), P("blk"))
    out_specs = P("blk", None)
    return jax.shard_map(shards, mesh=mesh, in_specs=in_specs, out_specs=out_specs, check_vma=False)
```

profile of v0, /device:TPU:0, one launch (start us, length us, event | category | flops | bytes accessed | tf_op | source)
XLA Modules:
  0.0 178.2 jit_solution(9994201577379634457)
XLA Ops:
  6.5 4.1 %collective-permute-start.4 = (bf16[768,256]{1,0:T(8,128)(2,1)}, bf16[768,256]{1,0:T(8,128)(2,1)S(1)}, u32[]{:S(2)}, u32[]{:S(2)}) collective-permute-start(bf16[768,256]{1,0:T(8,128)(2,1)} %param.4), channel_id=1, source_target_pairs={{0,8},{1,9},{2,10},{3,11},{4,12},{5,13},{6,14},{7,15},{8,0},{9,1},... | collective-permute-start | bytes 1179656 | tf_op jit(solution)/shard_map/ppermute | solution.py:15
  10.6 17.8 %collective-permute-done.4 = bf16[768,256]{1,0:T(8,128)(2,1)S(1)} collective-permute-done((bf16[768,256]{1,0:T(8,128)(2,1)}, bf16[768,256]{1,0:T(8,128)(2,1)S(1)}, u32[]{:S(2)}, u32[]{:S(2)}) %collective-permute-start.4) | collective-permute-done | bytes 393248 | tf_op jit(solution)/shard_map/ppermute | solution.py:15
  28.4 1.0 broadcast_select_fusion
  29.5 0.2 collective-permute-start.8
  29.7 5.0 %collective-permute-start.5 = (bf16[768,256]{1,0:T(8,128)(2,1)S(1)}, bf16[768,256]{1,0:T(8,128)(2,1)S(1)}, u32[]{:S(2)}, u32[]{:S(2)}) collective-permute-start(bf16[768,256]{1,0:T(8,128)(2,1)S(1)} %broadcast_select_fusion), channel_id=1, source_target_pairs={{0,4},{1,5},{2,6},{3,7},{4,8},{5,9},{6,10},{7,11},{8,12},{9,13},{1... | collective-permute-start | bytes 1179656 | tf_op jit(solution)/shard_map/ppermute | solution.py:15
  34.7 0.0 collective-permute-done.6
  34.7 5.6 %collective-permute-start.9 = (bf16[768]{0:T(1024)(128)(2,1)S(1)}, bf16[768]{0:T(1024)(128)(2,1)S(1)}, u32[]{:S(2)}, u32[]{:S(2)}) collective-permute-start(bf16[768]{0:T(1024)(128)(2,1)S(1)} %broadcast_select_fusion.1), channel_id=1, source_target_pairs={{0,3},{1,4},{2,5},{3,6},{4,7},{5,8},{6,9},{7,10},{8,11},{9,12},{10... | collective-permute-start | bytes 4616 | tf_op jit(solution)/shard_map/ppermute | solution.py:15
  40.4 3.7 %collective-permute-start.7 = (bf16[768]{0:T(1024)(128)(2,1)S(1)}, bf16[768]{0:T(1024)(128)(2,1)S(1)}, u32[]{:S(2)}, u32[]{:S(2)}) collective-permute-start(bf16[768]{0:T(1024)(128)(2,1)S(1)} %broadcast_select_fusion.1), channel_id=1, source_target_pairs={{0,4},{1,5},{2,6},{3,7},{4,8},{5,9},{6,10},{7,11},{8,12},{9,13},{1... | collective-permute-start | bytes 4616 | tf_op jit(solution)/shard_map/ppermute | solution.py:15
  44.1 0.2 multiply_reduce_fusion.4
  44.3 2.8 %collective-permute-done.9 = bf16[768]{0:T(1024)(128)(2,1)S(1)} collective-permute-done((bf16[768]{0:T(1024)(128)(2,1)S(1)}, bf16[768]{0:T(1024)(128)(2,1)S(1)}, u32[]{:S(2)}, u32[]{:S(2)}) %collective-permute-start.9) | collective-permute-done | bytes 1568 | tf_op jit(solution)/shard_map/ppermute | solution.py:15
  47.1 0.2 multiply_reduce_fusion.2
  47.3 0.2 multiply_reduce_fusion.3
  47.5 0.9 fusion.29
  48.4 0.9 fusion.30
  49.3 50.8 %while.20 = (s32[]{:T(128)}, f32[768,256]{1,0:T(8,128)S(1)}, bf16[768,256]{1,0:T(8,128)(2,1)S(1)}, bf16[768]{0:T(1024)(128)(2,1)S(1)}, bf16[768,256]{1,0:T(8,128...) while((s32[]{:T(128)}, f32[768,256]{1,0:T(8,128)S(1)}, ...), condition=%wide.region_6.7_spmd.clone.clone, body=%wide.region_3.6_spmd.clone.clone.sunk | while | flops 1217003520 | bytes 10276093 | solution.py:81
  49.4 6.5 %collective-permute-start = (bf16[768,256]{1,0:T(8,128)(2,1)S(1)}, bf16[768,256]{1,0:T(8,128)(2,1)S(1)}, u32[]{:S(2)}, u32[]{:S(2)}) collective-permute-start(bf16[768,256]{1,0:T(8,128)(2,1)S(1)} %get-tuple-element.178), channel_id=1, source_target_pairs={{0,15},{1,0},{2,1},{3,2},{4,3},{5,4},{6,5},{7,6},{8,7},{9,8},{10,9... | collective-permute-start | bytes 1179656 | tf_op jit(solution)/shard_map/while/body/eval_jaxpr/ppermute | solution.py:15
  55.8 4.4 %collective-permute-start.1 = (bf16[768]{0:T(1024)(128)(2,1)S(1)}, bf16[768]{0:T(1024)(128)(2,1)S(1)}, u32[]{:S(2)}, u32[]{:S(2)}) collective-permute-start(bf16[768]{0:T(1024)(128)(2,1)S(1)} %get-tuple-element.179), channel_id=1, source_target_pairs={{0,15},{1,0},{2,1},{3,2},{4,3},{5,4},{6,5},{7,6},{8,7},{9,8},{10,9... | collective-permute-start | bytes 4616 | tf_op jit(solution)/shard_map/while/body/eval_jaxpr/ppermute | solution.py:15
  60.3 1.3 collective-permute-done.1
  61.6 4.4 %collective-permute-done.3 = bf16[768]{0:T(1024)(128)(2,1)S(1)} collective-permute-done((bf16[768]{0:T(1024)(128)(2,1)S(1)}, bf16[768]{0:T(1024)(128)(2,1)S(1)}, u32[]{:S(2)}, u32[]{:S(2)}) %collective-permute-start.3) | collective-permute-done | bytes 1568 | tf_op jit(solution)/shard_map/while/body/eval_jaxpr/ppermute | solution.py:15
  66.0 0.2 multiply_reduce_fusion.7
  66.2 0.2 multiply_reduce_fusion.8
  66.5 1.8 %fusion.63 = f32[768,256]{1,0:T(8,128)} fusion(bf16[768,256]{1,0:T(8,128)(2,1)S(1)} %get-tuple-element.190, bf16[768,256]{1,0:T(8,128)(2,1)S(1)} %collective-permute-done, f32[768]{0:T(1024)S(1)} %multiply_reduce_fusion.7, f32[768]{0:T(1024)S(1)} %get-tuple-element.189, f32[768]{0:T(1024)S(1)} %convert_element_type.105), kind=kOutput, calls=%fused_computation.4.clone.1 | convolution fusion | flops 607715328 | bytes 1582080 | tf_op jit(solution)/shard_map/while/body/eval_jaxpr/dot_general | solution.py:48
  68.3 2.2 %fusion.64 = f32[768,256]{1,0:T(8,128)S(1)} fusion(f32[768,256]{1,0:T(8,128)} %fusion.63, f32[768,256]{1,0:T(8,128)S(1)} %get-tuple-element.175, bf16[768,256]{1,0:T(8,128)(2,1)S(1)} %get-tuple-element.190, bf16[768,256]{1,0:T(8,128)(2,1)S(1)} %collective-permute-done.2, f32[768]{0:T(1024)S(1)} %multiply_reduce_fusion.8, ...), kind=kOutput, calls=%fused_computation.6.clone.1 | convolution fusion | flops 608108544 | bytes 3154944 | tf_op jit(solution)/shard_map/while/body/eval_jaxpr/dot_general | solution.py:48
  70.5 0.1 collective-permute-start
  70.6 0.5 collective-permute-start.2
  71.1 4.0 %collective-permute-start.1 = (bf16[768]{0:T(1024)(128)(2,1)S(1)}, bf16[768]{0:T(1024)(128)(2,1)S(1)}, u32[]{:S(2)}, u32[]{:S(2)}) collective-permute-start(bf16[768]{0:T(1024)(128)(2,1)S(1)} %get-tuple-element.179), channel_id=1, source_target_pairs={{0,15},{1,0},{2,1},{3,2},{4,3},{5,4},{6,5},{7,6},{8,7},{9,8},{10,9... | collective-permute-start | bytes 4616 | tf_op jit(solution)/shard_map/while/body/eval_jaxpr/ppermute | solution.py:15
  75.1 1.3 collective-permute-done.1
  76.4 4.4 %collective-permute-done.3 = bf16[768]{0:T(1024)(128)(2,1)S(1)} collective-permute-done((bf16[768]{0:T(1024)(128)(2,1)S(1)}, bf16[768]{0:T(1024)(128)(2,1)S(1)}, u32[]{:S(2)}, u32[]{:S(2)}) %collective-permute-start.3) | collective-permute-done | bytes 1568 | tf_op jit(solution)/shard_map/while/body/eval_jaxpr/ppermute | solution.py:15
  80.9 0.2 multiply_reduce_fusion.7
  81.0 0.2 multiply_reduce_fusion.8
  81.3 1.8 %fusion.63 = f32[768,256]{1,0:T(8,128)} fusion(bf16[768,256]{1,0:T(8,128)(2,1)S(1)} %get-tuple-element.190, bf16[768,256]{1,0:T(8,128)(2,1)S(1)} %collective-permute-done, f32[768]{0:T(1024)S(1)} %multiply_reduce_fusion.7, f32[768]{0:T(1024)S(1)} %get-tuple-element.189, f32[768]{0:T(1024)S(1)} %convert_element_type.105), kind=kOutput, calls=%fused_computation.4.clone.1 | convolution fusion | flops 607715328 | bytes 1582080 | tf_op jit(solution)/shard_map/while/body/eval_jaxpr/dot_general | solution.py:48
  83.1 2.2 %fusion.64 = f32[768,256]{1,0:T(8,128)S(1)} fusion(f32[768,256]{1,0:T(8,128)} %fusion.63, f32[768,256]{1,0:T(8,128)S(1)} %get-tuple-element.175, bf16[768,256]{1,0:T(8,128)(2,1)S(1)} %get-tuple-element.190, bf16[768,256]{1,0:T(8,128)(2,1)S(1)} %collective-permute-done.2, f32[768]{0:T(1024)S(1)} %multiply_reduce_fusion.8, ...), kind=kOutput, calls=%fused_computation.6.clone.1 | convolution fusion | flops 608108544 | bytes 3154944 | tf_op jit(solution)/shard_map/while/body/eval_jaxpr/dot_general | solution.py:48
  85.3 0.1 collective-permute-start
  85.4 1.4 collective-permute-start.2
  86.9 3.0 %collective-permute-start.1 = (bf16[768]{0:T(1024)(128)(2,1)S(1)}, bf16[768]{0:T(1024)(128)(2,1)S(1)}, u32[]{:S(2)}, u32[]{:S(2)}) collective-permute-start(bf16[768]{0:T(1024)(128)(2,1)S(1)} %get-tuple-element.179), channel_id=1, source_target_pairs={{0,15},{1,0},{2,1},{3,2},{4,3},{5,4},{6,5},{7,6},{8,7},{9,8},{10,9... | collective-permute-start | bytes 4616 | tf_op jit(solution)/shard_map/while/body/eval_jaxpr/ppermute | solution.py:15
  89.9 1.3 collective-permute-done.1
  91.2 4.4 %collective-permute-done.3 = bf16[768]{0:T(1024)(128)(2,1)S(1)} collective-permute-done((bf16[768]{0:T(1024)(128)(2,1)S(1)}, bf16[768]{0:T(1024)(128)(2,1)S(1)}, u32[]{:S(2)}, u32[]{:S(2)}) %collective-permute-start.3) | collective-permute-done | bytes 1568 | tf_op jit(solution)/shard_map/while/body/eval_jaxpr/ppermute | solution.py:15
  95.7 0.2 multiply_reduce_fusion.7
  95.9 0.2 multiply_reduce_fusion.8
  96.1 1.8 %fusion.63 = f32[768,256]{1,0:T(8,128)} fusion(bf16[768,256]{1,0:T(8,128)(2,1)S(1)} %get-tuple-element.190, bf16[768,256]{1,0:T(8,128)(2,1)S(1)} %collective-permute-done, f32[768]{0:T(1024)S(1)} %multiply_reduce_fusion.7, f32[768]{0:T(1024)S(1)} %get-tuple-element.189, f32[768]{0:T(1024)S(1)} %convert_element_type.105), kind=kOutput, calls=%fused_computation.4.clone.1 | convolution fusion | flops 607715328 | bytes 1582080 | tf_op jit(solution)/shard_map/while/body/eval_jaxpr/dot_general | solution.py:48
  97.9 2.2 %fusion.64 = f32[768,256]{1,0:T(8,128)S(1)} fusion(f32[768,256]{1,0:T(8,128)} %fusion.63, f32[768,256]{1,0:T(8,128)S(1)} %get-tuple-element.175, bf16[768,256]{1,0:T(8,128)(2,1)S(1)} %get-tuple-element.190, bf16[768,256]{1,0:T(8,128)(2,1)S(1)} %collective-permute-done.2, f32[768]{0:T(1024)S(1)} %multiply_reduce_fusion.8, ...), kind=kOutput, calls=%fused_computation.6.clone.1 | convolution fusion | flops 608108544 | bytes 3154944 | tf_op jit(solution)/shard_map/while/body/eval_jaxpr/dot_general | solution.py:48
  100.2 0.0 copy-start.2
  100.2 0.9 copy-done.2
  101.0 0.0 all-reduce.3.cloned.1.call-update
  101.1 34.8 %all-reduce.3.cloned.1.call-done = f32[768,256]{1,0:T(8,128)} async-done(((f32[768,256]{1,0:T(8,128)}), f32[768,256]{1,0:T(8,128)}) %all-reduce.3.cloned.1.call-update) | async-done | bytes 786448 | tf_op jit(solution)/shard_map/psum | solution.py:87
  135.9 1.4 convert_reduce_fusion
  137.3 33.0 %all-reduce = (f32[256]{0:T(256)S(1)}, f32[256]{0:T(256)S(1)}) all-reduce(f32[256]{0:T(256)S(1)} %get-tuple-element.97, f32[256]{0:T(256)S(1)} %get-tuple-element.96), channel_id=1, replica_groups=mesh['layer'=2,'blk'=16] {'blk'}, use_global_device_ids=true, to_apply=%region_11.12 | all-reduce | flops 512 | bytes 4096 | tf_op jit(solution)/shard_map/psum | solution.py:89
  170.4 1.0 subtract_add_fusion
  (44 shorter events, 0.3 us)
Async XLA Ops:
  6.5 37.6 %copy-start.1 = (bf16[768,256]{1,0:T(8,128)(2,1)S(1)}, bf16[768,256]{1,0:T(8,128)(2,1)}, u32[]{:S(2)}) copy-start(bf16[768,256]{1,0:T(8,128)(2,1)} %param.4) | copy-start | bytes 1179652
  6.5 23.1 %copy-start.3 = (s32[768]{0:T(1024)S(1)}, s32[768]{0:T(1024)}, u32[]{:S(2)}) copy-start(s32[768]{0:T(1024)} %param.5) | copy-start | bytes 9220
  6.5 129.4 %all-reduce.3.cloned.1.call-start = ((), (), s32[]{:S(2)}) async-start(), calls=%async_computation | async-start | bytes 1572864 | tf_op jit(solution)/shard_map/psum | solution.py:87
  6.5 21.9 %collective-permute-start.4 = (bf16[768,256]{1,0:T(8,128)(2,1)}, bf16[768,256]{1,0:T(8,128)(2,1)S(1)}, u32[]{:S(2)}, u32[]{:S(2)}) collective-permute-start(bf16[768,256]{1,0:T(8,128)(2,1)} %param.4), channel_id=1, source_target_pairs={{0,8},{1,9},{2,10},{3,11},{4,12},{5,13},{6,14},{7,15},{8,0},{9,1},... | collective-permute-start | bytes 1179656 | tf_op jit(solution)/shard_map/ppermute | solution.py:15
  29.5 17.6 %collective-permute-start.8 = (bf16[768,256]{1,0:T(8,128)(2,1)S(1)}, bf16[768,256]{1,0:T(8,128)(2,1)S(1)}, u32[]{:S(2)}, u32[]{:S(2)}) collective-permute-start(bf16[768,256]{1,0:T(8,128)(2,1)S(1)} %broadcast_select_fusion), channel_id=1, source_target_pairs={{0,3},{1,4},{2,5},{3,6},{4,7},{5,8},{6,9},{7,10},{8,11},{9,12},{10... | collective-permute-start | bytes 1179656 | tf_op jit(solution)/shard_map/ppermute | solution.py:15
  29.7 5.1 %collective-permute-start.6 = (bf16[768]{0:T(1024)(128)(2,1)S(1)}, bf16[768]{0:T(1024)(128)(2,1)S(1)}, u32[]{:S(2)}, u32[]{:S(2)}) collective-permute-start(bf16[768]{0:T(1024)(128)(2,1)S(1)} %convert_element_type.52), channel_id=1, source_target_pairs={{0,8},{1,9},{2,10},{3,11},{4,12},{5,13},{6,14},{7,15},{8,0},{9,1},... | collective-permute-start | bytes 4616 | tf_op jit(solution)/shard_map/ppermute | solution.py:15
  29.7 17.6 %collective-permute-start.5 = (bf16[768,256]{1,0:T(8,128)(2,1)S(1)}, bf16[768,256]{1,0:T(8,128)(2,1)S(1)}, u32[]{:S(2)}, u32[]{:S(2)}) collective-permute-start(bf16[768,256]{1,0:T(8,128)(2,1)S(1)} %broadcast_select_fusion), channel_id=1, source_target_pairs={{0,4},{1,5},{2,6},{3,7},{4,8},{5,9},{6,10},{7,11},{8,12},{9,13},{1... | collective-permute-start | bytes 1179656 | tf_op jit(solution)/shard_map/ppermute | solution.py:15
  34.7 12.3 %collective-permute-start.9 = (bf16[768]{0:T(1024)(128)(2,1)S(1)}, bf16[768]{0:T(1024)(128)(2,1)S(1)}, u32[]{:S(2)}, u32[]{:S(2)}) collective-permute-start(bf16[768]{0:T(1024)(128)(2,1)S(1)} %broadcast_select_fusion.1), channel_id=1, source_target_pairs={{0,3},{1,4},{2,5},{3,6},{4,7},{5,8},{6,9},{7,10},{8,11},{9,12},{10... | collective-permute-start | bytes 4616 | tf_op jit(solution)/shard_map/ppermute | solution.py:15
  40.4 6.7 %collective-permute-start.7 = (bf16[768]{0:T(1024)(128)(2,1)S(1)}, bf16[768]{0:T(1024)(128)(2,1)S(1)}, u32[]{:S(2)}, u32[]{:S(2)}) collective-permute-start(bf16[768]{0:T(1024)(128)(2,1)S(1)} %broadcast_select_fusion.1), channel_id=1, source_target_pairs={{0,4},{1,5},{2,6},{3,7},{4,8},{5,9},{6,10},{7,11},{8,12},{9,13},{1... | collective-permute-start | bytes 4616 | tf_op jit(solution)/shard_map/ppermute | solution.py:15
  49.4 16.6 %collective-permute-start = (bf16[768,256]{1,0:T(8,128)(2,1)S(1)}, bf16[768,256]{1,0:T(8,128)(2,1)S(1)}, u32[]{:S(2)}, u32[]{:S(2)}) collective-permute-start(bf16[768,256]{1,0:T(8,128)(2,1)S(1)} %get-tuple-element.178), channel_id=1, source_target_pairs={{0,15},{1,0},{2,1},{3,2},{4,3},{5,4},{6,5},{7,6},{8,7},{9,8},{10,9... | collective-permute-start | bytes 1179656 | tf_op jit(solution)/shard_map/while/body/eval_jaxpr/ppermute | solution.py:15
  55.8 10.4 %collective-permute-start.2 = (bf16[768,256]{1,0:T(8,128)(2,1)S(1)}, bf16[768,256]{1,0:T(8,128)(2,1)S(1)}, u32[]{:S(2)}, u32[]{:S(2)}) collective-permute-start(bf16[768,256]{1,0:T(8,128)(2,1)S(1)} %get-tuple-element.176), channel_id=1, source_target_pairs={{0,1},{1,2},{2,3},{3,4},{4,5},{5,6},{6,7},{7,8},{8,9},{9,10},{10,1... | collective-permute-start | bytes 1179656 | tf_op jit(solution)/shard_map/while/body/eval_jaxpr/ppermute | solution.py:15
  55.8 5.7 %collective-permute-start.1 = (bf16[768]{0:T(1024)(128)(2,1)S(1)}, bf16[768]{0:T(1024)(128)(2,1)S(1)}, u32[]{:S(2)}, u32[]{:S(2)}) collective-permute-start(bf16[768]{0:T(1024)(128)(2,1)S(1)} %get-tuple-element.179), channel_id=1, source_target_pairs={{0,15},{1,0},{2,1},{3,2},{4,3},{5,4},{6,5},{7,6},{8,7},{9,8},{10,9... | collective-permute-start | bytes 4616 | tf_op jit(solution)/shard_map/while/body/eval_jaxpr/ppermute | solution.py:15
  60.3 5.7 %collective-permute-start.3 = (bf16[768]{0:T(1024)(128)(2,1)S(1)}, bf16[768]{0:T(1024)(128)(2,1)S(1)}, u32[]{:S(2)}, u32[]{:S(2)}) collective-permute-start(bf16[768]{0:T(1024)(128)(2,1)S(1)} %get-tuple-element.177), channel_id=1, source_target_pairs={{0,1},{1,2},{2,3},{3,4},{4,5},{5,6},{6,7},{7,8},{8,9},{9,10},{10,1... | collective-permute-start | bytes 4616 | tf_op jit(solution)/shard_map/while/body/eval_jaxpr/ppermute | solution.py:15
  70.5 10.3 %collective-permute-start = (bf16[768,256]{1,0:T(8,128)(2,1)S(1)}, bf16[768,256]{1,0:T(8,128)(2,1)S(1)}, u32[]{:S(2)}, u32[]{:S(2)}) collective-permute-start(bf16[768,256]{1,0:T(8,128)(2,1)S(1)} %get-tuple-element.178), channel_id=1, source_target_pairs={{0,15},{1,0},{2,1},{3,2},{4,3},{5,4},{6,5},{7,6},{8,7},{9,8},{10,9... | collective-permute-start | bytes 1179656 | tf_op jit(solution)/shard_map/while/body/eval_jaxpr/ppermute | solution.py:15
  70.6 10.4 %collective-permute-start.2 = (bf16[768,256]{1,0:T(8,128)(2,1)S(1)}, bf16[768,256]{1,0:T(8,128)(2,1)S(1)}, u32[]{:S(2)}, u32[]{:S(2)}) collective-permute-start(bf16[768,256]{1,0:T(8,128)(2,1)S(1)} %get-tuple-element.176), channel_id=1, source_target_pairs={{0,1},{1,2},{2,3},{3,4},{4,5},{5,6},{6,7},{7,8},{8,9},{9,10},{10,1... | collective-permute-start | bytes 1179656 | tf_op jit(solution)/shard_map/while/body/eval_jaxpr/ppermute | solution.py:15
  71.1 5.3 %collective-permute-start.1 = (bf16[768]{0:T(1024)(128)(2,1)S(1)}, bf16[768]{0:T(1024)(128)(2,1)S(1)}, u32[]{:S(2)}, u32[]{:S(2)}) collective-permute-start(bf16[768]{0:T(1024)(128)(2,1)S(1)} %get-tuple-element.179), channel_id=1, source_target_pairs={{0,15},{1,0},{2,1},{3,2},{4,3},{5,4},{6,5},{7,6},{8,7},{9,8},{10,9... | collective-permute-start | bytes 4616 | tf_op jit(solution)/shard_map/while/body/eval_jaxpr/ppermute | solution.py:15
  75.1 5.7 %collective-permute-start.3 = (bf16[768]{0:T(1024)(128)(2,1)S(1)}, bf16[768]{0:T(1024)(128)(2,1)S(1)}, u32[]{:S(2)}, u32[]{:S(2)}) collective-permute-start(bf16[768]{0:T(1024)(128)(2,1)S(1)} %get-tuple-element.177), channel_id=1, source_target_pairs={{0,1},{1,2},{2,3},{3,4},{4,5},{5,6},{6,7},{7,8},{8,9},{9,10},{10,1... | collective-permute-start | bytes 4616 | tf_op jit(solution)/shard_map/while/body/eval_jaxpr/ppermute | solution.py:15
  85.3 10.3 %collective-permute-start = (bf16[768,256]{1,0:T(8,128)(2,1)S(1)}, bf16[768,256]{1,0:T(8,128)(2,1)S(1)}, u32[]{:S(2)}, u32[]{:S(2)}) collective-permute-start(bf16[768,256]{1,0:T(8,128)(2,1)S(1)} %get-tuple-element.178), channel_id=1, source_target_pairs={{0,15},{1,0},{2,1},{3,2},{4,3},{5,4},{6,5},{7,6},{8,7},{9,8},{10,9... | collective-permute-start | bytes 1179656 | tf_op jit(solution)/shard_map/while/body/eval_jaxpr/ppermute | solution.py:15
  85.4 10.4 %collective-permute-start.2 = (bf16[768,256]{1,0:T(8,128)(2,1)S(1)}, bf16[768,256]{1,0:T(8,128)(2,1)S(1)}, u32[]{:S(2)}, u32[]{:S(2)}) collective-permute-start(bf16[768,256]{1,0:T(8,128)(2,1)S(1)} %get-tuple-element.176), channel_id=1, source_target_pairs={{0,1},{1,2},{2,3},{3,4},{4,5},{5,6},{6,7},{7,8},{8,9},{9,10},{10,1... | collective-permute-start | bytes 1179656 | tf_op jit(solution)/shard_map/while/body/eval_jaxpr/ppermute | solution.py:15
  86.9 4.3 %collective-permute-start.1 = (bf16[768]{0:T(1024)(128)(2,1)S(1)}, bf16[768]{0:T(1024)(128)(2,1)S(1)}, u32[]{:S(2)}, u32[]{:S(2)}) collective-permute-start(bf16[768]{0:T(1024)(128)(2,1)S(1)} %get-tuple-element.179), channel_id=1, source_target_pairs={{0,15},{1,0},{2,1},{3,2},{4,3},{5,4},{6,5},{7,6},{8,7},{9,8},{10,9... | collective-permute-start | bytes 4616 | tf_op jit(solution)/shard_map/while/body/eval_jaxpr/ppermute | solution.py:15
  89.9 5.7 %collective-permute-start.3 = (bf16[768]{0:T(1024)(128)(2,1)S(1)}, bf16[768]{0:T(1024)(128)(2,1)S(1)}, u32[]{:S(2)}, u32[]{:S(2)}) collective-permute-start(bf16[768]{0:T(1024)(128)(2,1)S(1)} %get-tuple-element.177), channel_id=1, source_target_pairs={{0,1},{1,2},{2,3},{3,4},{4,5},{5,6},{6,7},{7,8},{8,9},{9,10},{10,1... | collective-permute-start | bytes 4616 | tf_op jit(solution)/shard_map/while/body/eval_jaxpr/ppermute | solution.py:15
  100.2 0.9 copy-start.2
  135.9 34.5 %copy-start = (f32[768,256]{1,0:T(8,128)S(1)}, f32[768,256]{1,0:T(8,128)}, u32[]{:S(2)}) copy-start(f32[768,256]{1,0:T(8,128)} %all-reduce.3.cloned.1.call-done) | copy-start | bytes 2359300
Sparse Core Ops, SparseCore 0:
  101.2 34.6 all-reduce.2
where the time goes:
time: 179 us; the launch traced here: 178 us
  waiting for transfers between devices  72.6 us (41%)
  starting transfers between devices  38.7 us (22%)
  blocking collectives  33 us (18%)
  matrix products  14.1 us (8%)
  between operations  13.5 us (8%)
  other arithmetic  5.07 us (3%)
    ppermute x18, starting transfers between devices, from_behind(): lax.ppermute(x, axis, [(i, (i + by) % devices) for i in range(devices)])  38.7 us
    ppermute x18, waiting for transfers between devices, from_behind(): lax.ppermute(x, axis, [(i, (i + by) % devices) for i in range(devices)])  37.7 us
    psum x1, waiting for transfers between devices, shards(): row_sums = lax.psum(partial_value, 'layer')  34.8 us
    psum x1, blocking collectives, shards(): lax.psum((jnp.sum(member_f * row_sums, axis=0), jnp.sum(member_f, axis=0)...  33 us
    dot_general x8, matrix products, accumulate(): jnp.dot(kernel, onehot, preferred_element_type=jnp.float32)  14.1 us
  transfers between devices with their start and end apart: 19, of which 9 were waited for; matrix products, arithmetic and copies ran while one was open for 1% of the time, Pallas kernels for 0%

commit v1 on v0

v1 whole, which is shorter than its diff:
```python
import functools
import math

import jax
import jax.numpy as jnp
from jax import lax
from jax.experimental import pallas as pl
from jax.experimental.pallas import tpu as pltpu
from jax.sharding import PartitionSpec as P

K = 256
MESH = pl.DeviceIdType.MESH
NT = (((1,), (1,)), ((), ()))
CW, CCW = 0, 1
AUX, TX = 2, 3


def kernel(layers, nb, p_ref, lab_ref, out_ref, buf, aux, acc, mem_acc, rcol, lcol, own_aux, wsrc, wbuf,
           local_sem, ring_s, ring_r, d2d_s, d2d_r, x_s, x_r, w_s, w_r):
    rows, feat = p_ref.shape
    third = rows // 3
    groups = nb // 2
    far = groups // 2
    layer = lax.axis_index("layer")
    me = lax.axis_index("blk")
    core = me % 2
    group = me // 2
    low, odd = group // 2, group % 2
    place = low + odd * (groups - 1 - 2 * low)

    def group_at(pos):
        pos = (pos + groups) % groups
        side = pos // far
        return 2 * (pos + side * (groups - 1 - 2 * pos)) + side

    other_layer = layer + 1 - 2 * (layer % 2)
    side = layer % 2
    partner = 2 * group + 1 - core
    nexts = (2 * group_at(place + 1) + core, 2 * group_at(place - 1) + core)
    piece_x, piece_tx = 2 * side, 2 - 2 * side

    def from_at(way, d):
        return group_at(place - d) if way == CW else group_at(place + d)

    def ring_copy(src, way, d, item, device=None):
        return pltpu.make_async_remote_copy(
            src_ref=src, dst_ref=src, send_sem=ring_s.at[way, d, item], recv_sem=ring_r.at[way, d, item],
            device_id=(layer, nexts[way]), device_id_type=MESH)

    def d2d_copy(src, way, d, item):
        return pltpu.make_async_remote_copy(
            src_ref=src, dst_ref=src, send_sem=d2d_s.at[way, d, item], recv_sem=d2d_r.at[way, d, item],
            device_id=(layer, partner), device_id_type=MESH)

    def x_copy(src, way, d):
        return pltpu.make_async_remote_copy(
            src_ref=src, dst_ref=src, send_sem=x_s.at[way, d], recv_sem=x_r.at[way, d],
            device_id=(other_layer, me), device_id_type=MESH)

    own_load = [pltpu.make_async_copy(p_ref.at[pl.ds(t * third, third)], buf.at[me, t], local_sem.at[t])
                for t in range(3)]
    for copy in own_load:
        copy.start()

    barrier = pltpu.get_barrier_semaphore()

    def greet(o, carry):
        pl.semaphore_signal(barrier, inc=1, device_id=(layer, (me + o) % nb), device_id_type=MESH)
        return carry

    lax.fori_loop(1, nb, greet, 0)
    pl.semaphore_signal(barrier, inc=1, device_id=(other_layer, me), device_id_type=MESH)
    for copy in own_load:
        copy.wait()

    scale = math.log2(math.e) / feat
    for t in range(3):
        part = slice(t * third, (t + 1) * third)
        x = buf[me, t].astype(jnp.float32)
        sq = jnp.sum(x * x, axis=1, keepdims=True) * scale
        wide = jnp.broadcast_to(sq, (third, 128))
        rcol[part, :] = wide
        own_aux[:, part] = wide.T[0:1, :]
    lab = lab_ref[...].astype(jnp.float32)
    own_aux[:, rows:] = lab
    lcol[...] = jnp.broadcast_to(lab, (128, rows)).T
    acc[...] = jnp.zeros_like(acc)
    mem_acc[...] = jnp.zeros_like(mem_acc)
    pl.semaphore_wait(barrier, nb)

    def aux_send(way):
        return pltpu.make_async_remote_copy(
            src_ref=own_aux, dst_ref=aux.at[me], send_sem=ring_s.at[way, 1, AUX], recv_sem=ring_r.at[way, 1, AUX],
            device_id=(layer, nexts[way]), device_id_type=MESH)

    aux_d2d = pltpu.make_async_remote_copy(
        src_ref=own_aux, dst_ref=aux.at[me], send_sem=d2d_s.at[CW, 0, AUX], recv_sem=d2d_r.at[CW, 0, AUX],
        device_id=(layer, partner), device_id_type=MESH)

    for way in (CW, CCW):
        aux_send(way).start()
    ring_copy(buf.at[me, piece_x], CW, 1, 0).start()
    ring_copy(buf.at[me, 1], CCW, 1, 0).start()
    ring_copy(buf.at[me, 1], CW, 1, 1).start()
    ring_copy(buf.at[me, piece_x], CCW, 1, 1).start()
    aux_d2d.start()
    d2d_copy(buf.at[me], CW, 0, 0).start()

    ids = lax.broadcasted_iota(jnp.int32, (K, third), 0).astype(jnp.float32)
    own_copy = pltpu.make_async_copy(own_aux, aux.at[me], local_sem.at[0])
    own_copy.start()
    own_copy.wait()

    def visit(b, piece, offset):
        cols = buf[b, piece]
        col_sq = aux[b, :, pl.ds(offset, third)]
        tags = aux[b, :, pl.ds(pl.multiple_of(rows + offset, 128), third)]
        member = (tags == ids).astype(jnp.float32)
        mem_acc[...] += member
        member = member.astype(jnp.bfloat16)
        for r in range(3):
            part = slice(r * third, (r + 1) * third)
            gram = lax.dot_general(buf[me, r], cols, NT, preferred_element_type=jnp.float32)
            row_sq = rcol[part, :]
            row_sq = jnp.concatenate([row_sq] * (third // 128), axis=1)
            kern = jnp.exp2(gram * (2.0 * scale) - (row_sq + col_sq)).astype(jnp.bfloat16)
            acc[part, :] += lax.dot_general(kern, member, NT, preferred_element_type=jnp.float32)

    def see(b, piece):
        visit(b, piece, pl.multiple_of(piece * third, 128))

    def see_all(b):
        def one(t, carry):
            see(b, t)
            return carry
        lax.fori_loop(0, 3, one, 0)

    see_all(me)
    aux_d2d.wait_recv()
    d2d_copy(buf.at[partner], CW, 0, 0).wait_recv()
    see_all(partner)

    def ring_arrival(way, d, item, piece, onward, to_x):
        b = 2 * from_at(way, d) + core
        ref = buf.at[b, piece]
        ring_copy(ref, way, d, item).wait_recv()
        if onward:
            ring_copy(ref, way, d + 1, item).start()
        if to_x:
            x_copy(ref, way, d).start()
        d2d_copy(ref, way, d, item).start()

    def aux_arrival(way, d, onward):
        b = 2 * from_at(way, d) + core
        ref = aux.at[b]
        ring_copy(ref, way, d, AUX).wait_recv()
        if onward:
            ring_copy(ref, way, d + 1, AUX).start()
        d2d_copy(ref, way, d, AUX).start()

    def x_arrival(way, d, onward):
        b = 2 * from_at(way, d) + core
        ref = buf.at[b, piece_tx]
        x_copy(ref, way, d).wait_recv()
        if onward:
            ring_copy(ref, way, d + 1, TX).start()
        d2d_copy(ref, way, d, TX).start()

    def d2d_arrival(way, d, item, piece):
        b = 2 * from_at(way, d) + 1 - core
        ref = aux.at[b] if item == AUX else buf.at[b, piece]
        d2d_copy(ref, way, d, item).wait_recv()

    def see_list(entries):
        for way, d, item, piece in entries:
            see(2 * from_at(way, d) + core, piece)
        for way, d, item, piece in entries:
            d2d_arrival(way, d, item, piece)
            see(2 * from_at(way, d) + 1 - core, piece)

    def turn(d, with_x, last):
        for way in (CW, CCW):
            aux_arrival(way, d, onward=not last or way == CW)
        ring_arrival(CW, d, 0, piece_x, onward=True, to_x=True)
        ring_arrival(CCW, d, 0, 1, onward=True, to_x=False)
        if with_x:
            x_arrival(CW, d - 1, False)
        for way in (CW, CCW):
            d2d_arrival(way, d, AUX, None)
        entries = [(CW, d, 0, piece_x), (CCW, d, 0, 1)]
        if with_x:
            entries.append((CW, d - 1, TX, piece_tx))
        see_list(entries)
        ring_arrival(CW, d, 1, 1, onward=not last, to_x=False)
        ring_arrival(CCW, d, 1, piece_x, onward=not last, to_x=True)
        if with_x:
            x_arrival(CCW, d - 1, False)
        entries = [(CW, d, 1, 1), (CCW, d, 1, piece_x)]
        if with_x:
            entries.append((CCW, d - 1, TX, piece_tx))
        see_list(entries)

    turn(1, False, far == 2)
    if far > 3:
        lax.fori_loop(2, far - 1, lambda d, c: (turn(d, True, False), c)[1], 0)
    if far > 2:
        turn(far - 1, True, True)
    x_arrival(CW, far - 1, True)
    aux_arrival(CW, far, False)
    ring_arrival(CW, far, 0, piece_x, False, False)
    ring_arrival(CCW, far, 0, 1, False, False)
    d2d_arrival(CW, far, AUX, None)
    see_list([(CW, far - 1, TX, piece_tx), (CW, far, 0, piece_x), (CCW, far, 0, 1)])
    x_arrival(CCW, far - 1, False)
    see_list([(CCW, far - 1, TX, piece_tx)])
    ring_arrival(CW, far, TX, piece_tx, False, False)
    see_list([(CW, far, TX, piece_tx)])

    lane = lax.broadcasted_iota(jnp.int32, (rows, 128), 1).astype(jnp.float32)
    for h in range(K // 128):
        cut = slice(h * 128, (h + 1) * 128)
        mine = jnp.where(lcol[...] == lane + float(h * 128), acc[:, cut], 0.0)
        wsrc[:, cut] = jnp.sum(mine, axis=0, keepdims=True)

    def within_copy(o, sender):
        return pltpu.make_async_remote_copy(
            src_ref=wsrc, dst_ref=wbuf.at[sender], send_sem=w_s.at[o], recv_sem=w_r.at[o],
            device_id=(layer, (me + o) % nb), device_id_type=MESH)

    def send_within(o, carry):
        within_copy(o, me).start()
        return carry

    lax.fori_loop(1, nb, send_within, 0)
    ones = jnp.ones((8, K), jnp.bfloat16)
    counts = lax.dot_general(ones, mem_acc[...].astype(jnp.bfloat16).T, (((1,), (0,)), ((), ())),
                             preferred_element_type=jnp.float32)[0:1, :]
    factor = 2.0 / counts
    acc[...] = 1.0 - acc[...] * factor

    def drain(d):
        for way in (CW, CCW):
            for item in (0, 1):
                ring_copy(buf.at[me, 0], way, d, item).wait_send()
                d2d_copy(buf.at[me, 0], way, d, item).wait_send()
            ring_copy(aux.at[me], way, d, AUX).wait_send()
            d2d_copy(aux.at[me], way, d, AUX).wait_send()
            d2d_copy(buf.at[me, 0], way, d, TX).wait_send()
            x_copy(buf.at[me, 0], way, d).wait_send()

    lax.fori_loop(1, far, lambda d, c: (drain(d), c)[1], 0)
    ring_copy(buf.at[me, 0], CW, far, 0).wait_send()
    ring_copy(buf.at[me, 0], CCW, far, 0).wait_send()
    ring_copy(buf.at[me, 0], CW, far, TX).wait_send()
    ring_copy(aux.at[me], CW, far, AUX).wait_send()
    d2d_copy(buf.at[me, 0], CW, far, 0).wait_send()
    d2d_copy(buf.at[me, 0], CCW, far, 0).wait_send()
    d2d_copy(buf.at[me, 0], CW, far, TX).wait_send()
    d2d_copy(aux.at[me], CW, far, AUX).wait_send()
    d2d_copy(aux.at[me], CW, 0, AUX).wait_send()
    d2d_copy(buf.at[me], CW, 0, 0).wait_send()

    def wait_within(o, total):
        sender = (me - o + nb) % nb
        copy = within_copy(o, sender)
        copy.wait_recv()
        copy.wait_send()
        return total + wbuf[sender]

    within = lax.fori_loop(1, nb, wait_within, wsrc[...])
    out_ref[...] = acc[...] + within / (counts * counts)


def solution(mesh):
    layers, nb = mesh.shape["layer"], mesh.shape["blk"]

    def shards(points, labels):
        rows, feat = points.shape
        third = rows // 3
        far = nb // 4
        sems = pltpu.SemaphoreType.DMA
        return pl.pallas_call(
            functools.partial(kernel, layers, nb),
            out_shape=jax.ShapeDtypeStruct((rows, K), jnp.float32),
            in_specs=[pl.BlockSpec(memory_space=pl.ANY), pl.BlockSpec(memory_space=pltpu.VMEM)],
            out_specs=pl.BlockSpec(memory_space=pltpu.VMEM),
            scratch_shapes=[
                pltpu.VMEM((nb, 3, third, feat), jnp.bfloat16),
                pltpu.VMEM((nb, 1, 2 * rows), jnp.float32),
                pltpu.VMEM((rows, K), jnp.float32),
                pltpu.VMEM((K, third), jnp.float32),
                pltpu.VMEM((rows, 128), jnp.float32),
                pltpu.VMEM((rows, 128), jnp.float32),
                pltpu.VMEM((1, 2 * rows), jnp.float32),
                pltpu.VMEM((1, K), jnp.float32),
                pltpu.VMEM((nb, 1, K), jnp.float32),
                sems((3,)),
                sems((2, far + 1, 4)),
                sems((2, far + 1, 4)),
                sems((2, far + 1, 4)),
                sems((2, far + 1, 4)),
                sems((2, far + 1)),
                sems((2, far + 1)),
                sems((nb,)),
                sems((nb,)),
            ],
            compiler_params=pltpu.CompilerParams(
                collective_id=0, has_side_effects=True, vmem_limit_bytes=60 * 1024 * 1024),
        )(points, labels.reshape(1, rows))

    return jax.shard_map(
        shards, mesh=mesh, in_specs=(P("blk", None), P("blk")), out_specs=P("blk", None), check_vma=False)
```

time: 179 us -> 44.7 us (0.25)
  waiting for transfers between devices: 72.6 us -> 0 us
  Pallas kernels: 0 us -> 41.1 us
  starting transfers between devices: 38.7 us -> 0 us
  blocking collectives: 33 us -> 0 us
  matrix products: 14.1 us -> 0 us
  between operations: 13.5 us -> 0.01 us
  other arithmetic: 5.07 us -> 0 us
  local copies, waits for them, and re-layouts: 1.06 us -> 3.33 us
    pallas_call x0 -> x1, Pallas kernels: none -> 41.1 us  [shards(): pl.pallas_call(functools.partial(kernel, layers, nb), out_shape=jax.Shape...]
    ppermute x18 -> x0, starting transfers between devices: 38.7 us -> none  [from_behind(): lax.ppermute(x, axis, [(i, (i + by) % devices) for i in range(devices)])]
    ppermute x18 -> x0, waiting for transfers between devices: 37.7 us -> none  [from_behind(): lax.ppermute(x, axis, [(i, (i + by) % devices) for i in range(devices)])]
    psum x1 -> x0, waiting for transfers between devices: 34.8 us -> none  [shards(): row_sums = lax.psum(partial_value, 'layer')]
    psum x1 -> x0, blocking collectives: 33 us -> none  [shards(): lax.psum((jnp.sum(member_f * row_sums, axis=0), jnp.sum(member_f, axis=0)...]
    dot_general x8 -> x0, matrix products: 14.1 us -> none  [accumulate(): jnp.dot(kernel, onehot, preferred_element_type=jnp.float32)]
    reduce_sum x10 -> x0, other arithmetic: 3 us -> none  [the longest x1 1.41 us: shards(): jnp.sum(member_f, axis=0)]
  transfers between devices with their start and end apart: 19 -> 0, of which waited for: 9 -> 0; matrix products, arithmetic and copies ran while one was open for 1% -> 0% of each run, Pallas kernels for 0% -> 0%
where the time goes in v1:
time: 44.7 us; the launch traced here: 44.5 us
  Pallas kernels  41.1 us (92%)
  local copies, waits for them, and re-layouts  3.33 us (7%)
    pallas_call x1, Pallas kernels, shards(): pl.pallas_call(functools.partial(kernel, layers, nb), out_shape=jax.Shape...  41.1 us
    unnamed x1, local copies, waits for them, and re-layouts  2.06 us
    reshape x1, local copies, waits for them, and re-layouts, shards(): labels.reshape(1, rows)  1.27 us

profile of v1, /device:TPU:0, one launch (start us, length us, event | category | flops | bytes accessed | tf_op | source)
XLA Modules:
  0.0 44.5 jit_solution(18246724226254514876)
XLA Ops:
  0.0 1.3 %reshape.3.lab_ref = s32[1,768]{1,0:T(1,128)} reshape(s32[768]{0:T(1024)} %param.3) | data formatting | bytes 6144 | tf_op jit(solution)/shard_map/reshape | solution.py:309
  1.3 41.1 %shard_map.28 = f32[768,256]{1,0:T(8,128)} custom-call(bf16[768,256]{1,0:T(8,128)(2,1)} %p_ref.1, s32[1,768]{1,0:T(1,128)} %reshape.3.lab_ref), custom_call_target="tpu_custom_call" | custom-call | tf_op jit(solution)/shard_map/pallas_call | solution.py:282
  42.4 2.1 %copy.4 = f32[768,256]{1,0:T(8,128)} copy(f32[768,256]{1,0:T(8,128)} %shard_map.28) | data formatting | bytes 1572864

commit v2 on v1

--- a/solution.py
+++ b/solution.py
@@ -64,14 +64,15 @@
 
     barrier = pltpu.get_barrier_semaphore()
 
-    def greet(o, carry):
-        pl.semaphore_signal(barrier, inc=1, device_id=(layer, (me + o) % nb), device_id_type=MESH)
-        return carry
-
-    lax.fori_loop(1, nb, greet, 0)
-    pl.semaphore_signal(barrier, inc=1, device_id=(other_layer, me), device_id_type=MESH)
+    for place_of in ((layer, nexts[CW]), (layer, nexts[CCW]), (layer, partner), (other_layer, me)):
+        pl.semaphore_signal(barrier, inc=1, device_id=place_of, device_id_type=MESH)
     for copy in own_load:
         copy.wait()
+
+    pl.semaphore_wait(barrier, 4)
+    ring_copy(buf.at[me, piece_x], CW, 1, 0).start()
+    ring_copy(buf.at[me, 1], CCW, 1, 0).start()
+    d2d_copy(buf.at[me], CW, 0, 0).start()
 
     scale = math.log2(math.e) / feat
     for t in range(3):
@@ -81,12 +82,11 @@
         wide = jnp.broadcast_to(sq, (third, 128))
         rcol[part, :] = wide
         own_aux[:, part] = wide.T[0:1, :]
-    lab = lab_ref[...].astype(jnp.float32)
+    lab = lab_ref[...].reshape(1, rows).astype(jnp.float32)
     own_aux[:, rows:] = lab
     lcol[...] = jnp.broadcast_to(lab, (128, rows)).T
     acc[...] = jnp.zeros_like(acc)
     mem_acc[...] = jnp.zeros_like(mem_acc)
-    pl.semaphore_wait(barrier, nb)
 
     def aux_send(way):
         return pltpu.make_async_remote_copy(
@@ -99,12 +99,9 @@
 
     for way in (CW, CCW):
         aux_send(way).start()
-    ring_copy(buf.at[me, piece_x], CW, 1, 0).start()
-    ring_copy(buf.at[me, 1], CCW, 1, 0).start()
     ring_copy(buf.at[me, 1], CW, 1, 1).start()
     ring_copy(buf.at[me, piece_x], CCW, 1, 1).start()
     aux_d2d.start()
-    d2d_copy(buf.at[me], CW, 0, 0).start()
 
     ids = lax.broadcasted_iota(jnp.int32, (K, third), 0).astype(jnp.float32)
     own_copy = pltpu.make_async_copy(own_aux, aux.at[me], local_sem.at[0])
@@ -279,6 +276,7 @@
         third = rows // 3
         far = nb // 4
         sems = pltpu.SemaphoreType.DMA
+        vmem = nb * rows * feat * 2 + 16 * 1024 * 1024
         return pl.pallas_call(
             functools.partial(kernel, layers, nb),
             out_shape=jax.ShapeDtypeStruct((rows, K), jnp.float32),
@@ -305,8 +303,8 @@
                 sems((nb,)),
             ],
             compiler_params=pltpu.CompilerParams(
-                collective_id=0, has_side_effects=True, vmem_limit_bytes=60 * 1024 * 1024),
-        )(points, labels.reshape(1, rows))
+                collective_id=0, has_side_effects=True, vmem_limit_bytes=vmem),
+        )(points, labels)
 
     return jax.shard_map(
         shards, mesh=mesh, in_specs=(P("blk", None), P("blk")), out_specs=P("blk", None), check_vma=False)

time: 44.7 us -> 41.9 us (0.937)
  Pallas kernels: 41.1 us -> 39.2 us
  local copies, waits for them, and re-layouts: 3.33 us -> 2.56 us
    pallas_call x1, Pallas kernels: 41.1 us -> 39.2 us  [shards(): pl.pallas_call(functools.partial(kernel, layers, nb), out_shape=jax.Shape...]
    reshape x1 -> x0, local copies, waits for them, and re-layouts: 1.27 us -> none  [shards(): labels.reshape(1, rows)]
    unnamed x1 -> x5, local copies, waits for them, and re-layouts: 2.06 us -> 2.56 us
where the time goes in v2:
time: 41.9 us; the launch traced here: 41.7 us
  Pallas kernels  39.2 us (94%)
  local copies, waits for them, and re-layouts  2.56 us (6%)
    pallas_call x1, Pallas kernels, shards(): pl.pallas_call(functools.partial(kernel, layers, nb), out_shape=jax.Shape...  39.2 us
    unnamed x5, local copies, waits for them, and re-layouts  2.56 us

profile of v2, /device:TPU:0, one launch (start us, length us, event | category | flops | bytes accessed | tf_op | source)
XLA Modules:
  0.0 41.7 jit_solution(6591120856431334262)
XLA Ops:
  0.0 0.0 copy-start
  0.0 1.0 %copy-done = bf16[768,256]{1,0:T(8,128)(2,1)S(1)} copy-done((bf16[768,256]{1,0:T(8,128)(2,1)S(1)}, bf16[768,256]{1,0:T(8,128)(2,1)}, u32[]{:S(2)}) %copy-start) | copy-done | bytes 393240
  1.0 0.0 copy-start.1
  1.0 0.7 %copy-done.1 = s32[768]{0:T(1024)S(1)} copy-done((s32[768]{0:T(1024)S(1)}, s32[768]{0:T(1024)}, u32[]{:S(2)}) %copy-start.1) | copy-done | bytes 3096
  1.7 39.2 %shard_map.28 = f32[768,256]{1,0:T(8,128)S(1)} custom-call(bf16[768,256]{1,0:T(8,128)(2,1)S(1)} %copy-done, s32[768]{0:T(1024)S(1)} %copy-done.1), custom_call_target="tpu_custom_call" | custom-call | tf_op jit(solution)/shard_map/pallas_call | solution.py:280
  40.9 0.9 %copy.4 = f32[768,256]{1,0:T(8,128)} copy(f32[768,256]{1,0:T(8,128)S(1)} %shard_map.28) | data formatting | bytes 1572864
Async XLA Ops:
  0.0 1.0 %copy-start = (bf16[768,256]{1,0:T(8,128)(2,1)S(1)}, bf16[768,256]{1,0:T(8,128)(2,1)}, u32[]{:S(2)}) copy-start(bf16[768,256]{1,0:T(8,128)(2,1)} %p_ref.1) | copy-start | bytes 1179652
  1.0 0.7 %copy-start.1 = (s32[768]{0:T(1024)S(1)}, s32[768]{0:T(1024)}, u32[]{:S(2)}) copy-start(s32[768]{0:T(1024)} %lab_ref.1) | copy-start | bytes 9220

commit v3 on v2

--- a/solution.py
+++ b/solution.py
@@ -15,7 +15,7 @@
 AUX, TX = 2, 3
 
 
-def kernel(layers, nb, p_ref, lab_ref, out_ref, buf, aux, acc, mem_acc, rcol, lcol, own_aux, wsrc, wbuf,
+def kernel(layers, nb, p_ref, lab_ref, out_ref, buf, aux, acc, mem_acc, rcol, lcol, own_aux, wsrc, wbuf, wmine, wpeer,
            local_sem, ring_s, ring_r, d2d_s, d2d_r, x_s, x_r, w_s, w_r):
     rows, feat = p_ref.shape
     third = rows // 3
@@ -108,7 +108,7 @@
     own_copy.start()
     own_copy.wait()
 
-    def visit(b, piece, offset):
+    def visit(b, piece, offset, kind):
         cols = buf[b, piece]
         col_sq = aux[b, :, pl.ds(offset, third)]
         tags = aux[b, :, pl.ds(pl.multiple_of(rows + offset, 128), third)]
@@ -121,10 +121,10 @@
             row_sq = rcol[part, :]
             row_sq = jnp.concatenate([row_sq] * (third // 128), axis=1)
             kern = jnp.exp2(gram * (2.0 * scale) - (row_sq + col_sq)).astype(jnp.bfloat16)
-            acc[part, :] += lax.dot_general(kern, member, NT, preferred_element_type=jnp.float32)
+            acc[kind, part, :] += lax.dot_general(kern, member, NT, preferred_element_type=jnp.float32)
 
     def see(b, piece):
-        visit(b, piece, pl.multiple_of(piece * third, 128))
+        visit(b, piece, pl.multiple_of(piece * third, 128), piece)
 
     def see_all(b):
         def one(t, carry):
@@ -208,16 +208,20 @@
     ring_arrival(CCW, far, 0, 1, False, False)
     d2d_arrival(CW, far, AUX, None)
     see_list([(CW, far - 1, TX, piece_tx), (CW, far, 0, piece_x), (CCW, far, 0, 1)])
-    x_arrival(CCW, far - 1, False)
-    see_list([(CCW, far - 1, TX, piece_tx)])
-    ring_arrival(CW, far, TX, piece_tx, False, False)
-    see_list([(CW, far, TX, piece_tx)])
-
     lane = lax.broadcasted_iota(jnp.int32, (rows, 128), 1).astype(jnp.float32)
     for h in range(K // 128):
         cut = slice(h * 128, (h + 1) * 128)
-        mine = jnp.where(lcol[...] == lane + float(h * 128), acc[:, cut], 0.0)
-        wsrc[:, cut] = jnp.sum(mine, axis=0, keepdims=True)
+        mine = jnp.where(lcol[...] == lane + float(h * 128), acc[piece_x, :, cut] + 0.5 * acc[1, :, cut], 0.0)
+        wmine[:, cut] = jnp.sum(mine, axis=0, keepdims=True)
+
+    peer_copy = pltpu.make_async_remote_copy(
+        src_ref=wmine, dst_ref=wpeer, send_sem=w_s.at[0], recv_sem=w_r.at[0],
+        device_id=(other_layer, me), device_id_type=MESH)
+    peer_copy.start()
+    x_arrival(CCW, far - 1, False)
+    see_list([(CCW, far - 1, TX, piece_tx)])
+    peer_copy.wait()
+    wsrc[...] = wmine[...] + wpeer[...]
 
     def within_copy(o, sender):
         return pltpu.make_async_remote_copy(
@@ -229,11 +233,12 @@
         return carry
 
     lax.fori_loop(1, nb, send_within, 0)
+    ring_arrival(CW, far, TX, piece_tx, False, False)
+    see_list([(CW, far, TX, piece_tx)])
     ones = jnp.ones((8, K), jnp.bfloat16)
     counts = lax.dot_general(ones, mem_acc[...].astype(jnp.bfloat16).T, (((1,), (0,)), ((), ())),
                              preferred_element_type=jnp.float32)[0:1, :]
     factor = 2.0 / counts
-    acc[...] = 1.0 - acc[...] * factor
 
     def drain(d):
         for way in (CW, CCW):
@@ -265,7 +270,7 @@
         return total + wbuf[sender]
 
     within = lax.fori_loop(1, nb, wait_within, wsrc[...])
-    out_ref[...] = acc[...] + within / (counts * counts)
+    out_ref[...] = 1.0 + within / (counts * counts) - (acc[0] + acc[1] + acc[2]) * factor
 
 
 def solution(mesh):
@@ -285,13 +290,15 @@
             scratch_shapes=[
                 pltpu.VMEM((nb, 3, third, feat), jnp.bfloat16),
                 pltpu.VMEM((nb, 1, 2 * rows), jnp.float32),
-                pltpu.VMEM((rows, K), jnp.float32),
+                pltpu.VMEM((3, rows, K), jnp.float32),
                 pltpu.VMEM((K, third), jnp.float32),
                 pltpu.VMEM((rows, 128), jnp.float32),
                 pltpu.VMEM((rows, 128), jnp.float32),
                 pltpu.VMEM((1, 2 * rows), jnp.float32),
                 pltpu.VMEM((1, K), jnp.float32),
                 pltpu.VMEM((nb, 1, K), jnp.float32),
+                pltpu.VMEM((1, K), jnp.float32),
+                pltpu.VMEM((1, K), jnp.float32),
                 sems((3,)),
                 sems((2, far + 1, 4)),
                 sems((2, far + 1, 4)),

time: 41.9 us -> 43.6 us (1.041)
  Pallas kernels: 39.2 us -> 40.9 us
    pallas_call x1, Pallas kernels: 39.2 us -> 40.9 us  [shards(): pl.pallas_call(functools.partial(kernel, layers, nb), out_shape=jax.Shape...]
where the time goes in v3:
time: 43.6 us; the launch traced here: 43.5 us
  Pallas kernels  40.9 us (94%)
  local copies, waits for them, and re-layouts  2.56 us (6%)
    pallas_call x1, Pallas kernels, shards(): pl.pallas_call(functools.partial(kernel, layers, nb), out_shape=jax.Shape...  40.9 us
    unnamed x5, local copies, waits for them, and re-layouts  2.56 us

profile of v3, /device:TPU:0, one launch (start us, length us, event | category | flops | bytes accessed | tf_op | source)
XLA Modules:
  0.0 43.5 jit_solution(8705850086619126265)
XLA Ops:
  0.0 0.0 copy-start
  0.0 1.0 %copy-done = bf16[768,256]{1,0:T(8,128)(2,1)S(1)} copy-done((bf16[768,256]{1,0:T(8,128)(2,1)S(1)}, bf16[768,256]{1,0:T(8,128)(2,1)}, u32[]{:S(2)}) %copy-start) | copy-done | bytes 393240
  1.0 0.0 copy-start.1
  1.0 0.7 %copy-done.1 = s32[768]{0:T(1024)S(1)} copy-done((s32[768]{0:T(1024)S(1)}, s32[768]{0:T(1024)}, u32[]{:S(2)}) %copy-start.1) | copy-done | bytes 3096
  1.7 40.9 %shard_map.28 = f32[768,256]{1,0:T(8,128)S(1)} custom-call(bf16[768,256]{1,0:T(8,128)(2,1)S(1)} %copy-done, s32[768]{0:T(1024)S(1)} %copy-done.1), custom_call_target="tpu_custom_call" | custom-call | tf_op jit(solution)/shard_map/pallas_call | solution.py:285
  42.6 0.9 %copy.4 = f32[768,256]{1,0:T(8,128)} copy(f32[768,256]{1,0:T(8,128)S(1)} %shard_map.28) | data formatting | bytes 1572864
Async XLA Ops:
  0.0 1.0 %copy-start = (bf16[768,256]{1,0:T(8,128)(2,1)S(1)}, bf16[768,256]{1,0:T(8,128)(2,1)}, u32[]{:S(2)}) copy-start(bf16[768,256]{1,0:T(8,128)(2,1)} %p_ref.1) | copy-start | bytes 1179652
  1.0 0.7 %copy-start.1 = (s32[768]{0:T(1024)S(1)}, s32[768]{0:T(1024)}, u32[]{:S(2)}) copy-start(s32[768]{0:T(1024)} %lab_ref.1) | copy-start | bytes 9220
